TPU v7x, 32 devices: a whole 2x2x4 slice. The times are simulated.
32 devices in a mesh: expert: 16 (over z, y, core), tensor: 2 (over x).
Axes of the slice: x: 2, y: 2, z: 4, core: 2. Of those that a mesh axis runs over, the one named last changes fastest.
Arguments:
- tokens: bfloat16 [64, 256, 1280], P(('expert', 'tensor')), may hold values from -6 to 6
- slot_keys: bfloat16 [1280, 16], replicated, may hold values from -6 to 6
- logit_scale: float32 [], replicated, may hold values from 40 to 80
- w_in: bfloat16 [16, 1280, 3584], P('expert', None, 'tensor'), may hold values from -0.625 to 0.625
- b_in: bfloat16 [16, 3584], P('expert', 'tensor'), may hold values from -3 to 3
- w_out: bfloat16 [16, 3584, 1280], P('expert', 'tensor'), may hold values from -0.09375 to 0.09375
- b_out: bfloat16 [16, 1280], P('expert'), may hold values from -3 to 3
Outputs:
- mixed: bfloat16 [64, 256, 1280], P(('expert', 'tensor'))
All inputs are finite; a program needn't handle non-finite values.
Results may differ from a plain program's by a relative error of at most 0.0071.
Values may be sent and summed in bfloat16 or wider, within the bound.
A program may use at most 64 MiB of HBM per device.

v0:
```python
import jax
import jax.numpy as jnp
from jax import lax
from jax.sharding import PartitionSpec as P

EPS = 1e-06


def local(tokens, slot_keys, logit_scale, w_in, b_in, w_out, b_out):
    images, seq_len, width = tokens.shape
    slots = slot_keys.shape[1]
    row_sq = jnp.sum(jnp.square(tokens.astype(jnp.float32)), axis=2, keepdims=True)
    row_inv = lax.rsqrt(row_sq + EPS)
    key_sq = jnp.sum(jnp.square(slot_keys.astype(jnp.float32)), axis=0)
    key_inv = lax.rsqrt(key_sq + EPS)
    raw = jnp.dot(
        tokens.reshape(images * seq_len, width), slot_keys, preferred_element_type=jnp.float32
    )
    logits = logit_scale * row_inv * key_inv * raw.reshape(images, seq_len, slots)
    expo = jnp.exp(logits)
    dispatch = (expo / jnp.sum(expo, axis=1, keepdims=True)).astype(jnp.bfloat16)
    combine = (expo / jnp.sum(expo, axis=2, keepdims=True)).astype(jnp.bfloat16)
    slot_in = jnp.einsum(
        "ims,imd->isd", dispatch, tokens, preferred_element_type=jnp.float32
    ).astype(jnp.bfloat16)
    routed = lax.all_to_all(slot_in, "expert", split_axis=1, concat_axis=0, tiled=True)
    bias_wide = b_in.astype(jnp.float32)
    pre = (
        jnp.einsum(
            "rkd,kdf->rkf",
            lax.all_gather(routed, "tensor", axis=0, tiled=True),
            w_in,
            preferred_element_type=jnp.float32,
        )
        + bias_wide[None]
    )
    hidden = jax.nn.gelu(pre).astype(jnp.bfloat16)
    mine = lax.psum_scatter(
        jnp.einsum("rkf,kfd->rkd", hidden, w_out, preferred_element_type=jnp.float32),
        "tensor",
        scatter_dimension=0,
        tiled=True,
    )
    slot_out = (mine + b_out.astype(jnp.float32)[None]).astype(jnp.bfloat16)
    returned = lax.all_to_all(slot_out, "expert", split_axis=0, concat_axis=1, tiled=True)
    mixed = jnp.einsum("ims,isd->imd", combine, returned, preferred_element_type=jnp.float32)
    return mixed.astype(jnp.bfloat16)


def solution(mesh):
    placed = (
        P(("expert", "tensor"), None, None),
        P(),
        P(),
        P("expert", None, "tensor"),
        P("expert", "tensor"),
        P("expert", "tensor", None),
        P("expert", None),
    )
    return jax.shard_map(
        local,
        mesh=mesh,
        in_specs=placed,
        out_specs=P(("expert", "tensor"), None, None),
        check_vma=False,
    )
```

profile of v0, /device:TPU:0, one launch (start us, length us, event | category | flops | bytes accessed | tf_op | source)
XLA Modules:
  0.0 72.5 jit_solution(5864950734486424679)
XLA Ops:
  6.5 0.0 copy-start
  6.5 0.0 copy-start.1
  7.3 0.9 %multiply_reduce_fusion.1 = f32[16]{0:T(128)S(1)} fusion(bf16[1280,16]{0,1:T(8,128)(2,1)} %param.8), kind=kLoop, calls=%fused_computation.32 | loop fusion | flops 61424 | bytes 41024 | tf_op jit(solution)/shard_map/reduce_sum | solution.py:14
  8.2 1.7 %multiply_reduce_fusion = f32[2,256]{1,0:T(2,128)S(1)} fusion(bf16[2,256,1280]{2,1,0:T(8,128)(2,1)} %param.7), kind=kLoop, calls=%fused_computation.5 | loop fusion | flops 1965568 | bytes 1312768 | tf_op jit(solution)/shard_map/reduce_sum | solution.py:12
  9.9 1.8 %fusion.16 = f32[2,256,16]{1,2,0:T(8,128)S(1)} fusion(bf16[2,256,1280]{2,1,0:T(8,128)(2,1)} %param.7, bf16[1280,16]{0,1:T(8,128)(2,1)} %param.8, f32[16]{0:T(128)S(1)} %add_rsqrt_fusion, f32[2,256]{1,0:T(2,128)S(1)} %rsqrt_multiply_fusion), kind=kOutput, calls=%fused_computation.12 | convolution fusion | flops 20987904 | bytes 1386560 | tf_op jit(solution)/shard_map/dot_general | solution.py:16
  11.7 0.0 copy-done
  11.7 0.3 convolution_convert_fusion.1
  12.0 0.7 copy.13
  12.7 7.4 %all-to-all-start = ((bf16[2,16,1280]{2,0,1:T(2,128)(2,1)}), bf16[2,16,1280]{2,0,1:T(2,128)(2,1)S(1)}, u32[]{:S(2)}, u32[]{:S(2)}) async-start(bf16[2,16,1280]{2,0,1:T(2,128)(2,1)} %copy.13), calls=%async_computation | async-start | bytes 163840 | tf_op jit(solution)/shard_map/all_to_all | solution.py:26
  20.1 0.0 reduce-scatter.2.cloned.1.call-start
  20.2 0.0 copy-done.1
  20.2 7.0 %all-to-all-done = bf16[2,16,1280]{2,0,1:T(2,128)(2,1)S(1)} async-done(((bf16[2,16,1280]{2,0,1:T(2,128)(2,1)}), bf16[2,16,1280]{2,0,1:T(2,128)(2,1)S(1)}, u32[]{:S(2)}, u32[]{:S(2)}) %all-to-all-start) | async-done | bytes 81952 | tf_op jit(solution)/shard_map/all_to_all | solution.py:26
  27.3 5.1 %all_gather.3 = bf16[64,1,1280]{2,0,1:T(8,128)(2,1)S(1)} all-gather(bf16[32,1,1280]{2,0,1:T(8,128)(2,1)S(1)} %all_to_all.29), channel_id=1, replica_groups=mesh['expert'=16,'tensor'=2] {'tensor'}, dimensions={0}, use_global_device_ids=true | all-gather | bytes 245760 | tf_op jit(solution)/shard_map/all_gather | solution.py:31
  32.4 0.0 copy-start.2
  32.4 6.3 %fusion.4 = f32[64,1,1280]{2,0,1:T(8,128)} fusion(bf16[1,1792,1280]{2,1,0:T(8,128)(2,1)} %param.12, bf16[1,1280,1792]{2,1,0:T(8,128)(2,1)} %param.10, f32[1792]{0:T(1024)S(1)} %convert_reduce_fusion, bf16[64,1,1280]{2,0,1:T(8,128)(2,1)S(1)} %all_gather.3), kind=kOutput, calls=%fused_computation.6 | convolution fusion | flops 588349440 | bytes 9673728 | tf_op jit(solution)/shard_map/rkf,kfd->rkd/dot_general | solution.py:39
  38.7 0.0 reduce-scatter.2.cloned.1.call-update
  38.7 0.0 copy-done.2
  38.7 10.0 %reduce-scatter.2.cloned.1.call-done = f32[32,1,1280]{2,0,1:T(8,128)} async-done(((f32[64,1,1280]{2,0,1:T(8,128)}), f32[32,1,1280]{2,0,1:T(8,128)}) %reduce-scatter.2.cloned.1.call-update) | async-done | bytes 163856 | tf_op jit(solution)/shard_map/reduce_scatter | solution.py:38
  48.7 0.9 %add_convert_fusion = bf16[32,1,1280]{2,0,1:T(8,128)(2,1)S(1)} fusion(f32[32,1,1280]{2,0,1:T(8,128)} %reduce-scatter.2.cloned.1.call-done, f32[1280]{0:T(1024)S(1)} %convert_reduce_fusion.1), kind=kLoop, calls=%fused_computation.29 | loop fusion | flops 81920 | bytes 250880 | tf_op jit(solution)/shard_map/convert_element_type | solution.py:44
  49.7 0.5 broadcast.27
  50.2 0.7 reduce.5
  50.9 12.5 %all_to_all.36 = bf16[16,2,1280]{2,1,0:T(2,128)(2,1)S(1)} all-to-all(bf16[16,2,1280]{2,1,0:T(2,128)(2,1)S(1)} %reshape.50), channel_id=1, replica_groups=mesh['expert'=16,'tensor'=2] {'expert'}, dimensions={0} | all-to-all | bytes 163840 | tf_op jit(solution)/shard_map/all_to_all | solution.py:45
  63.4 0.1 reshape.51
  63.5 0.5 reduce.2
  64.0 1.6 %convolution_convert_fusion = bf16[2,256,1280]{2,1,0:T(8,128)(2,1)} fusion(bf16[16,2,1,1280]{3,1,0,2:T(2,128)(2,1)S(1)} %all_to_all.31, f32[2,256,16]{1,2,0:T(8,128)S(1)} %fusion.16), kind=kOutput, calls=%fused_computation.4 | convolution fusion | flops 21643792 | bytes 1425408 | tf_op jit(solution)/shard_map/ims,isd->imd/dot_general | solution.py:46
  (7 shorter events, 0.2 us)
Async XLA Ops:
  6.5 5.1 %copy-start = (bf16[2,256,1280]{2,1,0:T(8,128)(2,1)S(1)}, bf16[2,256,1280]{2,1,0:T(8,128)(2,1)}, u32[]{:S(2)}) copy-start(bf16[2,256,1280]{2,1,0:T(8,128)(2,1)} %param.7) | copy-start | bytes 3932164
  6.5 13.6 %copy-start.1 = (bf16[1,1792]{1,0:T(2,128)(2,1)S(1)}, bf16[1,1792]{1,0:T(2,128)(2,1)}, u32[]{:S(2)}) copy-start(bf16[1,1792]{1,0:T(2,128)(2,1)} %param.11) | copy-start | bytes 10756
  12.7 14.5 %all-to-all-start = ((bf16[2,16,1280]{2,0,1:T(2,128)(2,1)}), bf16[2,16,1280]{2,0,1:T(2,128)(2,1)S(1)}, u32[]{:S(2)}, u32[]{:S(2)}) async-start(bf16[2,16,1280]{2,0,1:T(2,128)(2,1)} %copy.13), calls=%async_computation | async-start | bytes 163840 | tf_op jit(solution)/shard_map/all_to_all | solution.py:26
  20.1 28.6 %reduce-scatter.2.cloned.1.call-start = ((), (), s32[]{:S(2)}) async-start(), calls=%async_computation.3 | async-start | bytes 491520 | tf_op jit(solution)/shard_map/reduce_scatter | solution.py:38
  32.4 6.3 %copy-start.2 = (bf16[1,1280]{1,0:T(2,128)(2,1)S(1)}, bf16[1,1280]{1,0:T(2,128)(2,1)}, u32[]{:S(2)}) copy-start(bf16[1,1280]{1,0:T(2,128)(2,1)} %param.13) | copy-start | bytes 7684
Sparse Core Ops, SparseCore 0:
  38.8 9.8 reduce-scatter.1
where the time goes:
time: 72.8 us; the launch traced here: 72.5 us
  blocking collectives  17.6 us (24%)
  waiting for transfers between devices  17.1 us (23%)
  between operations  14.3 us (20%)
  matrix products  9.99 us (14%)
  starting transfers between devices  7.46 us (10%)
  other arithmetic  4.67 us (6%)
  local copies, waits for them, and re-layouts  1.4 us (2%)
    all_to_all x1, blocking collectives, local(): lax.all_to_all(slot_out, 'expert', split_axis=0, concat_axis=1, tiled=True)  12.5 us
    reduce_scatter x1, waiting for transfers between devices, local(): lax.psum_scatter(jnp.einsum('rkf,kfd->rkd', hidden, w_out, preferred_elem...  10 us
    all_to_all x1, starting transfers between devices, local(): lax.all_to_all(slot_in, 'expert', split_axis=1, concat_axis=0, tiled=True)  7.41 us
    all_to_all x1, waiting for transfers between devices, local(): lax.all_to_all(slot_in, 'expert', split_axis=1, concat_axis=0, tiled=True)  7.02 us
    dot_general x1, matrix products, local(): jnp.einsum('rkf,kfd->rkd', hidden, w_out, preferred_element_type=jnp.floa...  6.26 us
    all_gather x1, blocking collectives, local(): lax.all_gather(routed, 'tensor', axis=0, tiled=True)  5.11 us
    dot_general x1, matrix products, local(): jnp.dot(tokens.reshape(images * seq_len, width), slot_keys, preferred_ele...  1.78 us
    reduce_sum x1, other arithmetic, local(): jnp.sum(jnp.square(tokens.astype(jnp.float32)), axis=2, keepdims=True)  1.65 us
  transfers between devices with their start and end apart: 2, of which 2 were waited for; matrix products, arithmetic and copies ran while one was open for 0% of the time, Pallas kernels for 0%

commit v1 on v0

--- a/solution.py
+++ b/solution.py
@@ -42,7 +42,10 @@
         tiled=True,
     )
     slot_out = (mine + b_out.astype(jnp.float32)[None]).astype(jnp.bfloat16)
-    returned = lax.all_to_all(slot_out, "expert", split_axis=0, concat_axis=1, tiled=True)
+    size = lax.axis_size("expert")
+    shards = jnp.stack(jnp.split(slot_out, size, axis=0), axis=0)
+    shards = lax.all_to_all(shards, "expert", split_axis=0, concat_axis=0)
+    returned = jnp.concatenate(shards, axis=1)
     mixed = jnp.einsum("ims,isd->imd", combine, returned, preferred_element_type=jnp.float32)
     return mixed.astype(jnp.bfloat16)
 

time: 72.8 us -> 71.3 us (0.979)
  other arithmetic: 4.67 us -> 3.55 us
    convert_element_type x2 -> x1, other arithmetic: 1.59 us -> 0.93 us  [local(): slot_out = (mine + b_out.astype(jnp.float32)[None]).astype(jnp.bfloat16)]
where the time goes in v1:
time: 71.3 us; the launch traced here: 71 us
  blocking collectives  17.6 us (25%)
  waiting for transfers between devices  17.1 us (24%)
  between operations  14.3 us (20%)
  matrix products  9.98 us (14%)
  starting transfers between devices  7.46 us (10%)
  other arithmetic  3.55 us (5%)
  local copies, waits for them, and re-layouts  1 us (1%)
    all_to_all x1, blocking collectives, local(): shards = lax.all_to_all(shards, 'expert', split_axis=0, concat_axis=0)  12.5 us
    reduce_scatter x1, waiting for transfers between devices, local(): lax.psum_scatter(jnp.einsum('rkf,kfd->rkd', hidden, w_out, preferred_elem...  10 us
    all_to_all x1, starting transfers between devices, local(): lax.all_to_all(slot_in, 'expert', split_axis=1, concat_axis=0, tiled=True)  7.41 us
    all_to_all x1, waiting for transfers between devices, local(): lax.all_to_all(slot_in, 'expert', split_axis=1, concat_axis=0, tiled=True)  7.02 us
    dot_general x1, matrix products, local(): jnp.einsum('rkf,kfd->rkd', hidden, w_out, preferred_element_type=jnp.floa...  6.26 us
    all_gather x1, blocking collectives, local(): lax.all_gather(routed, 'tensor', axis=0, tiled=True)  5.11 us
    dot_general x1, matrix products, local(): jnp.dot(tokens.reshape(images * seq_len, width), slot_keys, preferred_ele...  1.78 us
    reduce_sum x1, other arithmetic, local(): jnp.sum(jnp.square(tokens.astype(jnp.float32)), axis=2, keepdims=True)  1.65 us
  transfers between devices with their start and end apart: 2, of which 2 were waited for; matrix products, arithmetic and copies ran while one was open for 0% of the time, Pallas kernels for 0%

profile of v1, /device:TPU:0, one launch (start us, length us, event | category | flops | bytes accessed | tf_op | source)
XLA Modules:
  0.0 71.0 jit_solution(13144493296330274649)
XLA Ops:
  6.5 0.0 copy-start
  6.5 0.0 copy-start.1
  7.3 0.9 %multiply_reduce_fusion.1 = f32[16]{0:T(128)S(1)} fusion(bf16[1280,16]{0,1:T(8,128)(2,1)} %param.8), kind=kLoop, calls=%fused_computation.31 | loop fusion | flops 61424 | bytes 41024 | tf_op jit(solution)/shard_map/reduce_sum | solution.py:14
  8.2 1.7 %multiply_reduce_fusion = f32[2,256]{1,0:T(2,128)S(1)} fusion(bf16[2,256,1280]{2,1,0:T(8,128)(2,1)} %param.7), kind=kLoop, calls=%fused_computation.5 | loop fusion | flops 1965568 | bytes 1312768 | tf_op jit(solution)/shard_map/reduce_sum | solution.py:12
  9.9 1.8 %fusion.16 = f32[2,256,16]{1,2,0:T(8,128)S(1)} fusion(bf16[2,256,1280]{2,1,0:T(8,128)(2,1)} %param.7, bf16[1280,16]{0,1:T(8,128)(2,1)} %param.8, f32[16]{0:T(128)S(1)} %add_rsqrt_fusion, f32[2,256]{1,0:T(2,128)S(1)} %rsqrt_multiply_fusion), kind=kOutput, calls=%fused_computation.12 | convolution fusion | flops 20987904 | bytes 1386560 | tf_op jit(solution)/shard_map/dot_general | solution.py:16
  11.7 0.0 copy-done
  11.7 0.3 convolution_convert_fusion.1
  12.0 0.7 %copy.11 = bf16[2,16,1280]{2,0,1:T(2,128)(2,1)} copy(bf16[2,16,1280]{2,1,0:T(8,128)(2,1)S(1)} %convolution_convert_fusion.1) | data formatting | bytes 163840 | tf_op jit(solution)/shard_map/convert_element_type | solution.py:25
  12.7 7.4 %all-to-all-start = ((bf16[2,16,1280]{2,0,1:T(2,128)(2,1)}), bf16[2,16,1280]{2,0,1:T(2,128)(2,1)S(1)}, u32[]{:S(2)}, u32[]{:S(2)}) async-start(bf16[2,16,1280]{2,0,1:T(2,128)(2,1)} %copy.11), calls=%async_computation | async-start | bytes 163840 | tf_op jit(solution)/shard_map/all_to_all | solution.py:26
  20.1 0.0 reduce-scatter.2.cloned.1.call-start
  20.2 0.0 copy-done.1
  20.2 7.0 %all-to-all-done = bf16[2,16,1280]{2,0,1:T(2,128)(2,1)S(1)} async-done(((bf16[2,16,1280]{2,0,1:T(2,128)(2,1)}), bf16[2,16,1280]{2,0,1:T(2,128)(2,1)S(1)}, u32[]{:S(2)}, u32[]{:S(2)}) %all-to-all-start) | async-done | bytes 81952 | tf_op jit(solution)/shard_map/all_to_all | solution.py:26
  27.3 5.1 %all_gather.3 = bf16[64,1,1280]{2,0,1:T(8,128)(2,1)S(1)} all-gather(bf16[32,1,1280]{2,0,1:T(8,128)(2,1)S(1)} %all_to_all.19), channel_id=1, replica_groups=mesh['expert'=16,'tensor'=2] {'tensor'}, dimensions={0}, use_global_device_ids=true | all-gather | bytes 245760 | tf_op jit(solution)/shard_map/all_gather | solution.py:31
  32.4 0.0 copy-start.2
  32.4 6.3 %fusion.4 = f32[64,1,1280]{2,0,1:T(8,128)} fusion(bf16[1,1792,1280]{2,1,0:T(8,128)(2,1)} %param.12, bf16[1,1280,1792]{2,1,0:T(8,128)(2,1)} %param.10, f32[1792]{0:T(1024)S(1)} %convert_reduce_fusion, bf16[64,1,1280]{2,0,1:T(8,128)(2,1)S(1)} %all_gather.3), kind=kOutput, calls=%fused_computation.6 | convolution fusion | flops 588349440 | bytes 9673728 | tf_op jit(solution)/shard_map/rkf,kfd->rkd/dot_general | solution.py:39
  38.7 0.0 reduce-scatter.2.cloned.1.call-update
  38.7 0.0 copy-done.2
  38.7 10.0 %reduce-scatter.2.cloned.1.call-done = f32[32,1,1280]{2,0,1:T(8,128)} async-done(((f32[64,1,1280]{2,0,1:T(8,128)}), f32[32,1,1280]{2,0,1:T(8,128)}) %reduce-scatter.2.cloned.1.call-update) | async-done | bytes 163856 | tf_op jit(solution)/shard_map/reduce_scatter | solution.py:38
  48.7 0.9 %add_convert_fusion = bf16[32,1,1280]{2,0,1:T(8,128)(2,1)S(1)} fusion(f32[32,1,1280]{2,0,1:T(8,128)} %reduce-scatter.2.cloned.1.call-done, f32[1280]{0:T(1024)S(1)} %convert_reduce_fusion.1), kind=kLoop, calls=%fused_computation.29 | loop fusion | flops 81920 | bytes 250880 | tf_op jit(solution)/shard_map/convert_element_type | solution.py:44
  50.0 12.5 %all_to_all.23 = bf16[16,2,1,1280]{3,1,2,0:T(2,128)(2,1)S(1)} all-to-all(bf16[16,2,1,1280]{3,1,2,0:T(2,128)(2,1)S(1)} %constant_dynamic-update-slice_fusion), channel_id=1, replica_groups=mesh['expert'=16,'tensor'=2] {'expert'}, dimensions={0} | all-to-all | bytes 163840 | tf_op jit(solution)/shard_map/all_to_all | solution.py:47
  62.5 1.6 %convolution_convert_fusion = bf16[2,256,1280]{2,1,0:T(8,128)(2,1)} fusion(bf16[2,16,1280]{2,0,1:T(2,128)(2,1)S(1)} %bitcast.141, f32[2,256,16]{1,2,0:T(8,128)S(1)} %fusion.16), kind=kOutput, calls=%fused_computation.4 | convolution fusion | flops 21643792 | bytes 1425408 | tf_op jit(solution)/shard_map/ims,isd->imd/dot_general | solution.py:49
  (21 shorter events, 0.3 us)
Async XLA Ops:
  6.5 5.1 %copy-start = (bf16[2,256,1280]{2,1,0:T(8,128)(2,1)S(1)}, bf16[2,256,1280]{2,1,0:T(8,128)(2,1)}, u32[]{:S(2)}) copy-start(bf16[2,256,1280]{2,1,0:T(8,128)(2,1)} %param.7) | copy-start | bytes 3932164
  6.5 13.6 %copy-start.1 = (bf16[1,1792]{1,0:T(2,128)(2,1)S(1)}, bf16[1,1792]{1,0:T(2,128)(2,1)}, u32[]{:S(2)}) copy-start(bf16[1,1792]{1,0:T(2,128)(2,1)} %param.11) | copy-start | bytes 10756
  12.7 14.5 %all-to-all-start = ((bf16[2,16,1280]{2,0,1:T(2,128)(2,1)}), bf16[2,16,1280]{2,0,1:T(2,128)(2,1)S(1)}, u32[]{:S(2)}, u32[]{:S(2)}) async-start(bf16[2,16,1280]{2,0,1:T(2,128)(2,1)} %copy.11), calls=%async_computation | async-start | bytes 163840 | tf_op jit(solution)/shard_map/all_to_all | solution.py:26
  20.1 28.6 %reduce-scatter.2.cloned.1.call-start = ((), (), s32[]{:S(2)}) async-start(), calls=%async_computation.3 | async-start | bytes 491520 | tf_op jit(solution)/shard_map/reduce_scatter | solution.py:38
  32.4 6.3 %copy-start.2 = (bf16[1,1280]{1,0:T(2,128)(2,1)S(1)}, bf16[1,1280]{1,0:T(2,128)(2,1)}, u32[]{:S(2)}) copy-start(bf16[1,1280]{1,0:T(2,128)(2,1)} %param.13) | copy-start | bytes 7684
Sparse Core Ops, SparseCore 0:
  38.8 9.8 reduce-scatter.1
